TPU v7x, 32 devices: a whole 2x2x4 slice. The times are simulated.
32 devices in a mesh: tm: 8 (over y, x, core), chan: 4 (over z).
Axes of the slice: x: 2, y: 2, z: 4, core: 2. Of those that a mesh axis runs over, the one named last changes fastest.
Arguments:
- inputs: bfloat16 [4096, 8192], P('tm', 'chan'), may hold values from -52 to 52
- gate_logits: bfloat16 [4096, 8192], P(('tm', 'chan')), may hold values from -5 to 5
- step_sizes: bfloat16 [4096, 64], P('tm', 'chan'), may hold values from 0.3 to 28672, as said below
- decay_rates: float32 [8192], replicated, as said below
- skip_gain: float32 [8192], replicated, may hold values from 0.3 to 0.8
- norm_gain: float32 [8192], replicated, may hold values from 0.25 to 1.75
Outputs:
- outputs: bfloat16 [4096, 8192], P(('tm', 'chan'))
Inputs may be any that keep to these rules, and one draw needn't show every extreme that they name: `step_sizes`: every step size is positive. `decay_rates`: every rate is positive.
All inputs are finite; a program needn't handle non-finite values.
Results may differ from a plain program's by a relative error of at most 0.0049.
Values may be sent and summed in bfloat16 or wider, within the bound.
A program may use at most 64 MiB of HBM per device.

v0:
```python
import jax
import jax.numpy as jnp
from jax import lax
from jax.sharding import PartitionSpec as P

norm_epsilon = 1e-05


def entering(value, axis, combine, identity):
    count, mine = (lax.axis_size(axis), lax.axis_index(axis))
    everything = jax.tree.map(lambda part: lax.all_gather(part, axis), value)
    start = jax.tree.map(
        lambda part, zero: jnp.broadcast_to(jnp.asarray(zero, part.dtype), part.shape),
        value,
        identity,
    )

    def turn(k, before):
        reached = k < mine
        new = combine(before, jax.tree.map(lambda part: part[k], everything))
        return jax.tree.map(lambda a, b: jnp.where(reached, a, b), new, before)

    return lax.fori_loop(0, count, turn, start)


def combine_pairs(earlier, later):
    return (earlier[0] * later[0], later[0] * earlier[1] + later[1])


def widen(head_values, channels):
    head_count = head_values.shape[1]
    width_each = channels // head_count
    owner = lax.broadcasted_iota(jnp.int32, (head_count, channels), 1) // width_each
    column_head = lax.broadcasted_iota(jnp.int32, (head_count, channels), 0)
    spread_table = (owner == column_head).astype(jnp.float32)
    return jnp.dot(
        head_values,
        spread_table,
        precision=lax.Precision.HIGHEST,
        preferred_element_type=jnp.float32,
    )


def serial_rows(decays, drives, axis_pos):
    length = decays.shape[axis_pos]
    prod_list = []
    state_list = []
    prod_now = None
    state_now = None
    for index in range(length):
        decay_here = lax.index_in_dim(decays, index, axis_pos, keepdims=False)
        drive_here = lax.index_in_dim(drives, index, axis_pos, keepdims=False)
        if index == 0:
            prod_now = decay_here
            state_now = drive_here
        else:
            prod_now = prod_now * decay_here
            state_now = decay_here * state_now + drive_here
        prod_list.append(prod_now)
        state_list.append(state_now)
    return (jnp.stack(prod_list, axis=axis_pos), jnp.stack(state_list, axis=axis_pos))


def prefix_rows(decays, drives):
    length = decays.shape[0]
    channels = decays.shape[1]
    if length <= 8:
        return serial_rows(decays, drives, 0)
    group = 8
    groups = length // group
    grouped_decay = decays.reshape(groups, group, channels)
    grouped_drive = drives.reshape(groups, group, channels)
    inner_prod, inner_state = serial_rows(grouped_decay, grouped_drive, 1)
    outer_prod, outer_state = prefix_rows(inner_prod[:, -1, :], inner_state[:, -1, :])
    before_prod = jnp.concatenate([jnp.ones((1, channels), jnp.float32), outer_prod[:-1]], axis=0)
    before_state = jnp.concatenate(
        [jnp.zeros((1, channels), jnp.float32), outer_state[:-1]], axis=0
    )
    products = inner_prod * before_prod[:, None, :]
    states = inner_state + inner_prod * before_state[:, None, :]
    return (products.reshape(length, channels), states.reshape(length, channels))


def chain_time(end_decay, end_state):
    identity = (jnp.ones_like(end_decay), jnp.zeros_like(end_state))
    return entering((end_decay, end_state), "tm", combine_pairs, identity)[1]


def recurrence(block_inputs, block_steps, rates_here, skip_here, chain_fn):
    channels = block_inputs.shape[1]
    step_values = block_steps.astype(jnp.float32)
    widened = widen(step_values, channels) * rates_here[None, :]
    decays = jnp.exp(-widened)
    values = block_inputs.astype(jnp.float32)
    drives = jnp.sqrt(-jnp.expm1(-2.0 * widened)) * values
    products, local_states = prefix_rows(decays, drives)
    incoming = chain_fn(products[-1], local_states[-1])
    states = local_states + products * incoming[None, :]
    return (states + skip_here[None, :] * values).astype(jnp.bfloat16)


def normalize(mixed_rows, gate_logits, norm_gain):
    gated = mixed_rows.astype(jnp.float32) * jax.nn.silu(gate_logits.astype(jnp.float32))
    factor = lax.rsqrt(jnp.mean(gated * gated, axis=1, keepdims=True) + norm_epsilon)
    return (gated * factor * norm_gain[None, :]).astype(jnp.bfloat16)


def per_device(inputs, gate_logits, step_sizes, decay_rates, skip_gain, norm_gain):
    channels = inputs.shape[1]
    offset = lax.axis_index("chan") * channels
    rates_here = lax.dynamic_slice_in_dim(decay_rates, offset, channels, 0)
    skip_here = lax.dynamic_slice_in_dim(skip_gain, offset, channels, 0)
    mixed_rows = recurrence(inputs, step_sizes, rates_here, skip_here, chain_time)
    framed = lax.all_to_all(mixed_rows, "chan", split_axis=0, concat_axis=1, tiled=True)
    return normalize(framed, gate_logits, norm_gain)


def solution(mesh):
    in_specs = (P("tm", "chan"), P(("tm", "chan"), None), P("tm", "chan"), P(), P(), P())
    out_specs = P(("tm", "chan"), None)
    return jax.shard_map(
        per_device, mesh=mesh, in_specs=in_specs, out_specs=out_specs, check_vma=False
    )
```

profile of v0, /device:TPU:0, one launch (start us, length us, event | category | flops | bytes accessed | tf_op | source)
XLA Modules:
  0.0 148.7 jit_solution(7240075363780846964)
XLA Ops:
  0.0 0.0 copy-start
  0.0 0.7 dynamic_slice.20
  0.7 0.0 copy-done
  0.7 0.7 fusion.7
  1.5 0.0 copy-start.4
  1.5 0.9 exponential_bitcast_fusion
  2.4 0.6 copy-done.4
  3.1 2.7 %fusion = f32[64,8,2048]{2,1,0:T(8,128)S(1)} fusion(bf16[512,2048]{1,0:T(8,128)(2,1)S(1)} %copy-done.4, f32[2048,512]{0,1:T(8,128)S(1)} %fusion.7, f32[2048]{0:T(1024)S(1)} %dynamic_slice.20), kind=kLoop, calls=%fused_computation.7 | loop fusion | flops 5242880 | bytes 10493952 | tf_op jit(solution)/shard_map/reshape | solution.py:72
  5.8 6.3 %slice_multiply_fusion = (f32[64,1,2048]{2,1,0:T(1,128)S(1)}, f32[64,1,2048]{2,1,0:T(1,128)}, f32[64,1,2048]{2,1,0:T(1,128)}, f32[64,1,2048]{2,1,0:T(1,128)}, f3...) fusion(f32[64,8,2048]{2,1,0:T(8,128)S(1)} %exponential_bitcast_fusion), kind=kLoop, calls=%fused_computation.31 | loop fusion | flops 917504 | bytes 8388608 | tf_op jit(solution)/shard_map/mul | solution.py:57
  12.0 8.5 %slice_add_fusion = (f32[64,1,2048]{2,1,0:T(1,128)S(1)}, f32[64,1,2048]{2,1,0:T(1,128)}, f32[64,1,2048]{2,1,0:T(1,128)}, f32[64,1,2048]{2,1,0:T(1,128)}, f32[64,...) fusion(f32[64,8,2048]{2,1,0:T(8,128)S(1)} %fusion, ...), kind=kLoop, calls=%fused_computation.20 | loop fusion | flops 1835008 | bytes 12058624 | tf_op jit(solution)/shard_map/add | solution.py:58
  20.6 0.2 copy.19
  20.8 0.2 copy.18
  20.9 1.1 slice_multiply_fusion.7
  22.0 1.4 slice_add_fusion.7
  23.4 0.6 slice_bitcast_fusion.15
  24.0 0.1 fusion.13
  24.1 0.7 fusion.25
  24.8 2.3 %stack.10 = f32[8,8,2048]{2,1,0:T(8,128)} concatenate(f32[8,1,2048]{2,1,0:T(1,128)} %get-tuple-element.177, f32[8,1,2048]{2,1,0:T(1,128)} %get-tuple-element.153, f32[8,1,2048]{2,1,0:T(1,128)} %get-tuple-element.152, f32[8,1,2048]{2,1,0:T(1,128)} %get-tuple-element.151, f32[8,1,2048]{2,1,0:T(1,128)} %get-tuple-element.150, f32[8,1,2048]{2,1,0:T(1,128)} %get-tuple-element.149, ...), dimensions={1} | concatenate | bytes 1048576 | tf_op jit(solution)/shard_map/stack | solution.py:61
  27.1 2.2 %stack.11 = f32[8,8,2048]{2,1,0:T(8,128)} concatenate(f32[8,1,2048]{2,1,0:T(1,128)} %get-tuple-element.176, f32[8,1,2048]{2,1,0:T(1,128)} %get-tuple-element.146, f32[8,1,2048]{2,1,0:T(1,128)} %get-tuple-element.145, f32[8,1,2048]{2,1,0:T(1,128)} %get-tuple-element.144, f32[8,1,2048]{2,1,0:T(1,128)S(1)} %get-tuple-element.143, f32[8,1,2048]{2,1,0:T(1,128)S(1)} %get-tuple-element.142, ...), dimensions={1} | concatenate | bytes 1048576 | tf_op jit(solution)/shard_map/stack | solution.py:61
  29.3 0.8 concatenate.12
  30.1 0.9 concatenate.14
  31.0 1.3 multiply_bitcast_fusion.1
  32.3 0.8 concatenate.13
  33.1 0.8 concatenate.15
  34.0 11.9 %stack.8 = f32[64,8,2048]{2,1,0:T(8,128)} concatenate(f32[64,1,2048]{2,1,0:T(1,128)} %get-tuple-element.173, f32[64,1,2048]{2,1,0:T(1,128)} %get-tuple-element.167, f32[64,1,2048]{2,1,0:T(1,128)} %get-tuple-element.166, f32[64,1,2048]{2,1,0:T(1,128)} %get-tuple-element.165, f32[64,1,2048]{2,1,0:T(1,128)} %get-tuple-element.164, f32[64,1,2048]{2,1,0:T(1,128)} %get-tuple-element.163, ...), dimensions={1} | concatenate | bytes 8388608 | tf_op jit(solution)/shard_map/stack | solution.py:61
  45.9 0.0 copy-start.5
  45.9 12.0 %stack.9 = f32[64,8,2048]{2,1,0:T(8,128)} concatenate(f32[64,1,2048]{2,1,0:T(1,128)} %get-tuple-element.172, f32[64,1,2048]{2,1,0:T(1,128)} %get-tuple-element.160, f32[64,1,2048]{2,1,0:T(1,128)} %get-tuple-element.159, f32[64,1,2048]{2,1,0:T(1,128)} %get-tuple-element.158, f32[64,1,2048]{2,1,0:T(1,128)} %get-tuple-element.157, f32[64,1,2048]{2,1,0:T(1,128)} %get-tuple-element.156, ...), dimensions={1} | concatenate | bytes 8388608 | tf_op jit(solution)/shard_map/stack | solution.py:61
  57.8 0.0 copy-done.5
  57.8 0.0 dynamic-slice-start
  57.8 5.6 %multiply_bitcast_fusion = (f32[512,2048]{1,0:T(8,128)S(1)}, f32[512,2048]{1,0:T(8,128)S(1)}) fusion(f32[64,8,2048]{2,1,0:T(8,128)} %stack.9, f32[64,2048]{1,0:T(8,128)} %concatenate.15, f32[64,8,2048]{2,1,0:T(8,128)} %stack.8, f32[64,2048]{1,0:T(8,128)S(1)} %copy-done.5), kind=kLoop, calls=%fused_computation.17 | loop fusion | flops 3145728 | bytes 17825792 | tf_op jit(solution)/shard_map/mul | solution.py:79
  63.5 0.0 copy-start.1
  63.5 0.0 copy-start.2
  63.5 10.7 %all-gather.1 = f32[8,1,2048]{2,1,0:T(1,128)S(1)} all-gather(f32[1,1,2048]{2,1,0:T(1,128)S(1)} %slice_bitcast_fusion), channel_id=1, replica_groups=mesh['tm'=8,'chan'=4] {'tm'}, dimensions={0}, use_global_device_ids=true | all-gather | bytes 73728 | tf_op jit(solution)/shard_map/all_gather | solution.py:11
  74.3 0.0 copy-done.1
  74.3 0.0 copy-done.2
  74.3 9.2 %all-gather = f32[8,1,2048]{2,1,0:T(1,128)S(1)} all-gather(f32[1,1,2048]{2,1,0:T(1,128)S(1)} %slice_bitcast_fusion.1), channel_id=1, replica_groups=mesh['tm'=8,'chan'=4] {'tm'}, dimensions={0}, use_global_device_ids=true | all-gather | bytes 73728 | tf_op jit(solution)/shard_map/all_gather | solution.py:11
  83.6 0.7 while.14
  84.3 0.0 dynamic-slice-done
  84.3 4.7 %fusion.2 = bf16[512,2048]{1,0:T(8,128)(2,1)S(1)} fusion(bf16[512,2048]{1,0:T(8,128)(2,1)S(1)} %copy-done.4, f32[512,2048]{1,0:T(8,128)} %copy-done.2, f32[512,2048]{1,0:T(8,128)} %copy-done.1, f32[2048]{0:T(1024)S(1)} %dynamic-slice-done, f32[2048]{0:T(1024)S(1)} %get-tuple-element.99), kind=kLoop, calls=%fused_computation.9 | loop fusion | flops 6291456 | bytes 12599296 | tf_op jit(solution)/shard_map/convert_element_type | solution.py:99
  89.0 53.4 %all_to_all.13 = bf16[4,128,2048]{2,1,0:T(8,128)(2,1)S(1)} all-to-all(bf16[4,128,2048]{2,1,0:T(8,128)(2,1)S(1)} %bitcast.133), channel_id=1, replica_groups=mesh['tm'=8,'chan'=4] {'chan'}, dimensions={0} | all-to-all | bytes 4194304 | tf_op jit(solution)/shard_map/all_to_all | solution.py:114
  142.4 0.5 convert_bitcast_fusion
  142.9 0.0 copy-start.3
  142.9 0.3 copy.13
  143.2 0.0 copy-start.6
  143.2 1.3 copy-done.3
  144.5 1.5 multiply_reduce_fusion
  145.9 0.0 copy-done.6
  146.0 2.8 %multiply_convert_fusion = bf16[128,8192]{1,0:T(8,128)(2,1)} fusion(f32[8192]{0:T(1024)S(1)} %copy-done.6, f32[128]{0:T(128)S(1)} %add_rsqrt_fusion, f32[128,8192]{1,0:T(8,128)S(1)} %bitcast.132, bf16[128,8192]{1,0:T(8,128)(2,1)S(1)} %copy-done.3), kind=kLoop, calls=%fused_computation.15 | loop fusion | flops 9437184 | bytes 8421888 | tf_op jit(solution)/shard_map/convert_element_type | solution.py:105
  (27 shorter events, 0.3 us)
Async XLA Ops:
  0.0 0.7 copy-start
  1.5 1.6 %copy-start.4 = (bf16[512,2048]{1,0:T(8,128)(2,1)S(1)}, bf16[512,2048]{1,0:T(8,128)(2,1)}, u32[]{:S(2)}) copy-start(bf16[512,2048]{1,0:T(8,128)(2,1)} %param.8) | copy-start | bytes 6291460
  45.9 12.0 %copy-start.5 = (f32[64,2048]{1,0:T(8,128)S(1)}, f32[64,2048]{1,0:T(8,128)}, u32[]{:S(2)}) copy-start(f32[64,2048]{1,0:T(8,128)} %concatenate.13) | copy-start | bytes 1572868
  57.8 26.5 %dynamic-slice-start = ((f32[8192]{0:T(1024)}, s32[]{:T(128)}), f32[2048]{0:T(1024)S(1)}, s32[]{:S(2)}) async-start(f32[8192]{0:T(1024)} %param.12, s32[]{:T(128)} %select_n.32), calls=%async_computation.1 | async-start | bytes 16896 | tf_op jit(solution)/shard_map/dynamic_slice | solution.py:112
  63.5 10.8 %copy-start.1 = (f32[512,2048]{1,0:T(8,128)}, f32[512,2048]{1,0:T(8,128)S(1)}, u32[]{:S(2)}) copy-start(f32[512,2048]{1,0:T(8,128)S(1)} %get-tuple-element.170) | copy-start | bytes 12582916
  63.5 10.8 %copy-start.2 = (f32[512,2048]{1,0:T(8,128)}, f32[512,2048]{1,0:T(8,128)S(1)}, u32[]{:S(2)}) copy-start(f32[512,2048]{1,0:T(8,128)S(1)} %get-tuple-element.171) | copy-start | bytes 12582916
  142.9 1.6 %copy-start.3 = (bf16[128,8192]{1,0:T(8,128)(2,1)S(1)}, bf16[128,8192]{1,0:T(8,128)(2,1)}, u32[]{:S(2)}) copy-start(bf16[128,8192]{1,0:T(8,128)(2,1)} %param.9) | copy-start | bytes 6291460
  143.2 2.8 %copy-start.6 = (f32[8192]{0:T(1024)S(1)}, f32[8192]{0:T(1024)}, u32[]{:S(2)}) copy-start(f32[8192]{0:T(1024)} %param.13) | copy-start | bytes 98308
where the time goes:
time: 152 us; the launch traced here: 149 us
  blocking collectives  73.3 us (48%)
  other arithmetic  38.1 us (25%)
  local copies, waits for them, and re-layouts  35.8 us (24%)
    all_to_all x1, blocking collectives, per_device(): lax.all_to_all(mixed_rows, 'chan', split_axis=0, concat_axis=1, tiled=True)  53.4 us
    all_gather x2, blocking collectives, entering(): everything = jax.tree.map(lambda part: lax.all_gather(part, axis), value)  20 us
    another operation x2, local copies, waits for them, and re-layouts, serial_rows(): jnp.stack(prod_list, axis=axis_pos)  14.2 us
    another operation x2, local copies, waits for them, and re-layouts, serial_rows(): jnp.stack(state_list, axis=axis_pos)  14.2 us
    add x3, other arithmetic, serial_rows(): state_now = decay_here * state_now + drive_here  10 us
    mul x3, other arithmetic, serial_rows(): prod_now = prod_now * decay_here  8 us
    mul x2, other arithmetic, prefix_rows(): products = inner_prod * before_prod[:, None, :]  6.93 us
    convert_element_type x1, other arithmetic, recurrence(): return (states + skip_here[None, :] * values).astype(jnp.bfloat16)  4.67 us

commit v1 on v0

v1 whole, which is shorter than its diff:
```python
import functools

import jax
import jax.numpy as jnp
from jax import lax
from jax.experimental import pallas as pl
from jax.experimental.pallas import tpu as pltpu
from jax.sharding import PartitionSpec as P

norm_epsilon = 1e-05
MESH = pl.DeviceIdType.MESH
LANES = 128
ROWS = 8
CHUNKS = 4
EARLY = 2


def order_table(tokens):
    run = tokens // ROWS
    row = lax.broadcasted_iota(jnp.int32, (tokens, tokens), 0)
    col = lax.broadcasted_iota(jnp.int32, (tokens, tokens), 1)
    return ((row % ROWS) * run + row // ROWS == col).astype(jnp.float32).astype(jnp.bfloat16)


def head_steps(steps, head, rate):
    heads = steps.shape[1]
    pick = lax.broadcasted_iota(jnp.int32, (heads, LANES), 0) == head
    table = pick.astype(jnp.float32).astype(jnp.bfloat16)
    return jnp.dot(steps, table, preferred_element_type=jnp.float32) * rate


def decay_and_scale(widened):
    decay = jnp.exp(-widened)
    twice = widened + widened
    series = twice * (1.0 + twice * (twice * (1.0 / 6.0) - 0.5))
    kept = jnp.where(twice < 0.0625, series, 1.0 - decay * decay)
    scale = kept * lax.rsqrt(jnp.maximum(kept, 1e-37))
    return decay, scale


def across_rows(prod, state):
    row = lax.broadcasted_iota(jnp.int32, prod.shape, 0)
    step = 1
    while step < ROWS:
        before_prod = jnp.where(row < step, 1.0, pltpu.roll(prod, step, 0))
        before_state = jnp.where(row < step, 0.0, pltpu.roll(state, step, 0))
        state = prod * before_state + state
        prod = prod * before_prod
        step *= 2
    return prod, state


def kernel(
    x_hbm, gate_hbm, steps_ref, rates_ref, skip_ref, gain_ref,
    out_ref,
    gated_all, x_loc, gate, recv, order, steps_in, steps_order, steps_mine,
    tot_prod, tot_state, block_out, block_in, carry_out, carry_in, sums, sums_plain,
    load_sem, x_send, x_recv, step_send, step_recv, block_send, block_recv, carry_send, carry_recv,
    *, tm_count, chan_count,
):
    me_tm = lax.axis_index("tm")
    me = lax.axis_index("chan")
    channels = x_loc.shape[1]
    heads = channels // LANES
    rows = gate.shape[0]
    run = rows // ROWS
    width = channels // CHUNKS
    chunk_heads = heads // CHUNKS

    load_x = pltpu.make_async_copy(x_hbm, x_loc, load_sem.at[0])
    load_own = pltpu.make_async_copy(x_hbm.at[pl.ds(me * rows, rows)], recv.at[me], load_sem.at[1])
    load_gate = pltpu.make_async_copy(gate_hbm, gate, load_sem.at[2])
    load_x.start()
    barrier = pltpu.get_barrier_semaphore()
    for d in range(1, chan_count):
        pl.semaphore_signal(
            barrier, 1, device_id={"chan": lax.rem(me + d, chan_count)}, device_id_type=MESH
        )

    def greet(k, _):
        pl.semaphore_signal(
            barrier, 1, device_id={"tm": lax.rem(me_tm + k, tm_count)}, device_id_type=MESH
        )
        return 0

    lax.fori_loop(1, tm_count, greet, 0)
    load_own.start()
    load_gate.start()

    order[...] = order_table(rows)
    def order_steps(steps):
        return lax.dot_general(
            order[...], steps, (((1,), (1,)), ((), ())), preferred_element_type=jnp.float32
        ).astype(jnp.bfloat16)

    for i in range(chan_count):
        steps_mine[i] = order_steps(steps_ref[:, i * rows:(i + 1) * rows])

    def x_copy(s, d):
        peer = lax.rem(me + d, chan_count)
        cols = pl.ds(pl.multiple_of(s * width, width), width)
        return pltpu.make_async_remote_copy(
            src_ref=x_loc.at[pl.ds(pl.multiple_of(peer * rows, rows), rows), cols],
            dst_ref=recv.at[me, :, cols],
            send_sem=x_send.at[s, d],
            recv_sem=x_recv.at[s, d],
            device_id={"chan": peer},
            device_id_type=MESH,
        )

    def step_copy(d):
        peer = lax.rem(me + d, chan_count)
        return pltpu.make_async_remote_copy(
            src_ref=steps_ref.at[:, pl.ds(pl.multiple_of(peer * rows, rows), rows)],
            dst_ref=steps_in.at[me],
            send_sem=step_send.at[d], recv_sem=step_recv.at[d],
            device_id={"chan": peer}, device_id_type=MESH,
        )

    def carry_copy(d):
        peer = lax.rem(me + d, chan_count)
        return pltpu.make_async_remote_copy(
            src_ref=carry_out.at[peer], dst_ref=carry_in.at[me],
            send_sem=carry_send.at[d], recv_sem=carry_recv.at[d],
            device_id={"chan": peer}, device_id_type=MESH,
        )

    def block_copy(k):
        return pltpu.make_async_remote_copy(
            src_ref=block_out, dst_ref=block_in.at[me_tm],
            send_sem=block_send.at[k], recv_sem=block_recv.at[k],
            device_id={"tm": lax.rem(me_tm + k, tm_count)}, device_id_type=MESH,
        )

    load_x.wait()
    pl.semaphore_wait(barrier, tm_count - 1 + chan_count - 1)
    for d in range(1, chan_count):
        x_copy(0, d).start()
    for d in range(1, chan_count):
        step_copy(d).start()
    for s in range(1, EARLY):
        for d in range(1, chan_count):
            x_copy(s, d).start()

    def total_head(head, _):
        cols = pl.ds(pl.multiple_of(head * LANES, LANES), LANES)
        rate = rates_ref[pl.ds(me * heads + head, 1), :]
        block_prod = jnp.ones((1, LANES), jnp.float32)
        block_state = jnp.zeros((1, LANES), jnp.float32)
        for i in range(chan_count):
            values = jnp.dot(
                order[...], x_loc[i * rows:(i + 1) * rows, cols],
                preferred_element_type=jnp.float32,
            )
            widened = head_steps(steps_mine[i], head, rate)
            prod = state = None
            for j in range(run):
                here = slice(j * ROWS, (j + 1) * ROWS)
                decay, scale = decay_and_scale(widened[here])
                drive = scale * values[here]
                prod = decay if j == 0 else prod * decay
                state = drive if j == 0 else decay * state + drive
            prod, state = across_rows(prod, state)
            last_prod, last_state = prod[ROWS - 1:], state[ROWS - 1:]
            tot_prod[i, :, cols] = last_prod
            tot_state[i, :, cols] = last_state
            block_state = last_prod * block_state + last_state
            block_prod = block_prod * last_prod
        block_out[0, :, cols] = block_prod
        block_out[1, :, cols] = block_state
        return 0

    lax.fori_loop(0, heads, total_head, 0)

    def send_block(k, _):
        block_copy(k).start()
        return 0

    lax.fori_loop(1, tm_count, send_block, 0)
    block_in[me_tm] = block_out[...]
    load_own.wait()
    load_gate.wait()
    sums[...] = jnp.zeros_like(sums)

    def take_block(k, _):
        block_copy(k).wait()
        return 0

    lax.fori_loop(1, tm_count, take_block, 0)

    def fold(k, carried):
        new = block_in[k, 0] * carried + block_in[k, 1]
        return jnp.where(k < me_tm, new, carried)

    carried = lax.fori_loop(0, tm_count, fold, jnp.zeros((1, channels), jnp.float32))
    for i in range(chan_count):
        carry_out[i] = carried
        carried = tot_prod[i] * carried + tot_state[i]
    carry_in[me] = carry_out[me]
    for d in range(1, chan_count):
        carry_copy(d).start()
    for s in range(EARLY, CHUNKS):
        for d in range(1, chan_count):
            x_copy(s, d).start()

    def state_head(source, head):
        cols = pl.ds(pl.multiple_of(head * LANES, LANES), LANES)
        whole = source * heads + head
        wide_cols = pl.ds(pl.multiple_of(whole * LANES, LANES), LANES)
        rate = rates_ref[pl.ds(whole, 1), :]
        skip = skip_ref[pl.ds(whole, 1), :]
        carried = carry_in[source, :, cols]
        values = jnp.dot(order[...], recv[source, :, cols], preferred_element_type=jnp.float32)
        logits = jnp.dot(order[...], gate[:, wide_cols], preferred_element_type=jnp.float32)
        widened = head_steps(steps_order[source], head, rate)
        prods, states = [], []
        for j in range(run):
            here = slice(j * ROWS, (j + 1) * ROWS)
            decay, scale = decay_and_scale(widened[here])
            drive = scale * values[here]
            prods.append(decay if j == 0 else prods[-1] * decay)
            states.append(drive if j == 0 else decay * states[-1] + drive)
        prod, state = across_rows(prods[-1], states[-1])
        ends = state + prod * carried
        row = lax.broadcasted_iota(jnp.int32, ends.shape, 0)
        entering = jnp.where(row < 1, carried, pltpu.roll(ends, 1, 0))
        for j in range(run):
            here = slice(j * ROWS, (j + 1) * ROWS)
            mixed = states[j] + prods[j] * entering + skip * values[here]
            mixed = mixed.astype(jnp.bfloat16).astype(jnp.float32)
            logit = logits[here]
            gated = mixed * (logit * (0.5 + 0.5 * jnp.tanh(0.5 * logit)))
            gated_all[whole, pl.ds(j, ROWS, stride=run), :] = gated
            sums[here, :] += gated * gated

    steps_order[me] = order_steps(steps_ref[:, pl.ds(pl.multiple_of(me * rows, rows), rows)])

    def own_head(head, _):
        state_head(me, head)
        return 0

    lax.fori_loop(0, heads, own_head, 0)
    for d in range(1, chan_count):
        step_copy(d).wait()
        carry_copy(d).wait()
        source = lax.rem(me + chan_count - d, chan_count)
        steps_order[source] = order_steps(steps_in[source])

    def arrive(t, _):
        s = t // (chan_count - 1)
        d = t % (chan_count - 1) + 1
        x_copy(s, d).wait_recv()
        source = lax.rem(me + chan_count - d, chan_count)

        def one(h, _):
            state_head(source, s * chunk_heads + h)
            return 0

        lax.fori_loop(0, chunk_heads, one, 0)
        return 0

    lax.fori_loop(0, CHUNKS * (chan_count - 1), arrive, 0)

    for j in range(run):
        sums_plain[pl.ds(j, ROWS, stride=run), :] = sums[j * ROWS:(j + 1) * ROWS, :]
    mean = jnp.sum(sums_plain[...], axis=1, keepdims=True) * (1.0 / gate.shape[1])
    factor = jnp.broadcast_to(lax.rsqrt(mean + norm_epsilon), sums_plain.shape)

    def finish(head, _):
        cols = pl.ds(pl.multiple_of(head * LANES, LANES), LANES)
        gain = gain_ref[pl.ds(head, 1), :]
        out_ref[:, cols] = (gated_all[head] * factor * gain).astype(out_ref.dtype)
        return 0

    lax.fori_loop(0, gate.shape[1] // LANES, finish, 0)

    def sent(t, _):
        x_copy(t // (chan_count - 1), t % (chan_count - 1) + 1).wait_send()
        return 0

    lax.fori_loop(0, CHUNKS * (chan_count - 1), sent, 0)


def per_device(tm_count, chan_count, inputs, gate_logits, step_sizes, decay_rates, skip_gain, norm_gain):
    tokens, channels = inputs.shape
    rows, width = gate_logits.shape
    heads = channels // LANES
    f32, bf16 = jnp.float32, jnp.bfloat16
    vmem = pl.BlockSpec(memory_space=pltpu.VMEM)
    hbm = pl.BlockSpec(memory_space=pl.ANY)
    dma = pltpu.SemaphoreType.DMA
    return pl.pallas_call(
        functools.partial(kernel, tm_count=tm_count, chan_count=chan_count),
        out_shape=jax.ShapeDtypeStruct((rows, width), bf16),
        in_specs=[hbm, hbm, vmem, vmem, vmem, vmem],
        out_specs=vmem,
        scratch_shapes=[
            pltpu.VMEM((width // LANES, rows, LANES), f32),
            pltpu.VMEM((tokens, channels), bf16),
            pltpu.VMEM((rows, width), bf16),
            pltpu.VMEM((chan_count, rows, channels), bf16),
            pltpu.VMEM((rows, rows), bf16),
            pltpu.VMEM((chan_count, heads, rows), bf16),
            pltpu.VMEM((chan_count, rows, heads), bf16),
            pltpu.VMEM((chan_count, rows, heads), bf16),
            pltpu.VMEM((chan_count, 1, channels), f32),
            pltpu.VMEM((chan_count, 1, channels), f32),
            pltpu.VMEM((2, 1, channels), f32),
            pltpu.VMEM((tm_count, 2, 1, channels), f32),
            pltpu.VMEM((chan_count, 1, channels), f32),
            pltpu.VMEM((chan_count, 1, channels), f32),
            pltpu.VMEM((rows, LANES), f32),
            pltpu.VMEM((rows, LANES), f32),
            dma((3,)),
            dma((CHUNKS, chan_count)),
            dma((CHUNKS, chan_count)),
            dma((chan_count,)),
            dma((chan_count,)),
            dma((tm_count,)),
            dma((tm_count,)),
            dma((chan_count,)),
            dma((chan_count,)),
        ],
        compiler_params=pltpu.CompilerParams(
            collective_id=0, has_side_effects=True, vmem_limit_bytes=56 * 1024 * 1024
        ),
    )(
        inputs, gate_logits, step_sizes.T,
        decay_rates.reshape(-1, LANES), skip_gain.reshape(-1, LANES), norm_gain.reshape(-1, LANES),
    )


def solution(mesh):
    in_specs = (P("tm", "chan"), P(("tm", "chan"), None), P("tm", "chan"), P(), P(), P())
    out_specs = P(("tm", "chan"), None)
    body = functools.partial(per_device, mesh.shape["tm"], mesh.shape["chan"])
    return jax.shard_map(
        body, mesh=mesh, in_specs=in_specs, out_specs=out_specs, check_vma=False
    )
```

time: 152 us -> 63.8 us (0.42); the launches traced: 149 us -> 63.6 us
  blocking collectives: 73.3 us -> 0 us
  Pallas kernels: 0 us -> 60.5 us
  other arithmetic: 38.1 us -> 0 us
  local copies, waits for them, and re-layouts: 35.8 us -> 3.1 us
    pallas_call x0 -> x1, Pallas kernels: none -> 60.5 us  [per_device(): pl.pallas_call(functools.partial(kernel, tm_count=tm_count, chan_count=ch...]
    all_to_all x1 -> x0, blocking collectives: 53.4 us -> none  [per_device(): lax.all_to_all(mixed_rows, 'chan', split_axis=0, concat_axis=1, tiled=True)]
    another operation x6 -> x0, local copies, waits for them, and re-layouts: 28.4 us -> none  [the longest x2 14.2 us: serial_rows(): jnp.stack(prod_list, axis=axis_pos)]
    all_gather x2 -> x0, blocking collectives: 20 us -> none  [entering(): everything = jax.tree.map(lambda part: lax.all_gather(part, axis), value)]
    mul x5 -> x0, other arithmetic: 14.9 us -> none  [the longest x3 8 us: serial_rows(): prod_now = prod_now * decay_here]
    add x3 -> x0, other arithmetic: 10 us -> none  [serial_rows(): state_now = decay_here * state_now + drive_here]
    convert_element_type x2 -> x0, other arithmetic: 7.44 us -> none  [the longest x1 4.67 us: recurrence(): return (states + skip_here[None, :] * values).astype(jnp.bfloat16)]
    reshape x2 -> x0, other arithmetic: 3.66 us -> none  [the longest x1 2.72 us: prefix_rows(): grouped_drive = drives.reshape(groups, group, channels)]
where the time goes in v1:
time: 63.8 us; the launch traced here: 63.6 us
  Pallas kernels  60.5 us (95%)
  local copies, waits for them, and re-layouts  3.1 us (5%)
    pallas_call x1, Pallas kernels, per_device(): pl.pallas_call(functools.partial(kernel, tm_count=tm_count, chan_count=ch...  60.5 us
    unnamed x1, local copies, waits for them, and re-layouts  3.1 us

profile of v1, /device:TPU:0, one launch (start us, length us, event | category | flops | bytes accessed | tf_op | source)
XLA Modules:
  0.0 63.6 jit_solution(9546661977626263576)
XLA Ops:
  0.0 60.5 %shard_map.64 = bf16[128,8192]{1,0:T(8,128)(2,1)} custom-call(bf16[512,2048]{1,0:T(8,128)(2,1)} %x_hbm.1, bf16[128,8192]{1,0:T(8,128)(2,1)} %gate_hbm.1, bf16[16,512]{1,0:T(8,128)(2,1)} %bitcast.7, f32[64,128]{1,0:T(8,128)} %bitcast.4, f32[64,128]{1,0:T(8,128)} %bitcast.5, f32[64,128]{1,0:T(8,128)} %bitcast.6), custom_call_target="tpu_custom_call" | custom-call | tf_op jit(solution)/shard_map/pallas_call | solution.py:292
  60.5 3.1 %copy.8 = bf16[128,8192]{1,0:T(8,128)(2,1)} copy(bf16[128,8192]{1,0:T(8,128)(2,1)} %shard_map.64) | data formatting | bytes 4194304

commit v2 on v1

--- a/solution.py
+++ b/solution.py
@@ -13,6 +13,7 @@
 ROWS = 8
 CHUNKS = 4
 EARLY = 2
+FINISH = 8
 
 
 def order_table(tokens):
@@ -52,9 +53,10 @@
 
 def kernel(
     x_hbm, gate_hbm, steps_ref, rates_ref, skip_ref, gain_ref,
-    out_ref,
-    gated_all, x_loc, gate, recv, order, steps_in, steps_order, steps_mine,
+    gated_all, factor_ref,
+    x_loc, gate, recv, order, steps_in, steps_order, steps_mine,
     tot_prod, tot_state, block_out, block_in, carry_out, carry_in, sums, sums_plain,
+    decays, scales, prods, silus,
     load_sem, x_send, x_recv, step_send, step_recv, block_send, block_recv, carry_send, carry_recv,
     *, tm_count, chan_count,
 ):
@@ -203,37 +205,64 @@
         for d in range(1, chan_count):
             x_copy(s, d).start()
 
-    def state_head(source, head):
-        cols = pl.ds(pl.multiple_of(head * LANES, LANES), LANES)
+    def places(source, head):
         whole = source * heads + head
-        wide_cols = pl.ds(pl.multiple_of(whole * LANES, LANES), LANES)
+        return (
+            whole,
+            pl.ds(pl.multiple_of(head * LANES, LANES), LANES),
+            pl.ds(pl.multiple_of(whole * LANES, LANES), LANES),
+        )
+
+    def prepare_head(source, head):
+        whole, _, wide_cols = places(source, head)
         rate = rates_ref[pl.ds(whole, 1), :]
-        skip = skip_ref[pl.ds(whole, 1), :]
-        carried = carry_in[source, :, cols]
-        values = jnp.dot(order[...], recv[source, :, cols], preferred_element_type=jnp.float32)
         logits = jnp.dot(order[...], gate[:, wide_cols], preferred_element_type=jnp.float32)
         widened = head_steps(steps_order[source], head, rate)
-        prods, states = [], []
+        prod = None
         for j in range(run):
             here = slice(j * ROWS, (j + 1) * ROWS)
             decay, scale = decay_and_scale(widened[here])
-            drive = scale * values[here]
-            prods.append(decay if j == 0 else prods[-1] * decay)
-            states.append(drive if j == 0 else decay * states[-1] + drive)
-        prod, state = across_rows(prods[-1], states[-1])
+            prod = decay if j == 0 else prod * decay
+            logit = logits[here]
+            decays[whole, here, :] = decay
+            scales[whole, here, :] = scale
+            prods[whole, here, :] = prod
+            silus[whole, here, :] = logit * (0.5 + 0.5 * jnp.tanh(0.5 * logit))
+
+    def state_head(source, head):
+        whole, cols, _ = places(source, head)
+        skip = skip_ref[pl.ds(whole, 1), :]
+        gain = gain_ref[pl.ds(whole, 1), :]
+        carried = carry_in[source, :, cols]
+        values = jnp.dot(order[...], recv[source, :, cols], preferred_element_type=jnp.float32)
+        states = []
+        for j in range(run):
+            here = slice(j * ROWS, (j + 1) * ROWS)
+            drive = scales[whole, here, :] * values[here]
+            states.append(drive if j == 0 else decays[whole, here, :] * states[-1] + drive)
+        prod, state = across_rows(prods[whole, (run - 1) * ROWS:, :], states[-1])
         ends = state + prod * carried
         row = lax.broadcasted_iota(jnp.int32, ends.shape, 0)
         entering = jnp.where(row < 1, carried, pltpu.roll(ends, 1, 0))
         for j in range(run):
             here = slice(j * ROWS, (j + 1) * ROWS)
-            mixed = states[j] + prods[j] * entering + skip * values[here]
-            mixed = mixed.astype(jnp.bfloat16).astype(jnp.float32)
-            logit = logits[here]
-            gated = mixed * (logit * (0.5 + 0.5 * jnp.tanh(0.5 * logit)))
-            gated_all[whole, pl.ds(j, ROWS, stride=run), :] = gated
+            mixed = states[j] + prods[whole, here, :] * entering + skip * values[here]
+            gated = mixed.astype(jnp.bfloat16).astype(jnp.float32) * silus[whole, here, :]
+            gated_all[whole, pl.ds(j, ROWS, stride=run), :] = gated * gain
             sums[here, :] += gated * gated
 
     steps_order[me] = order_steps(steps_ref[:, pl.ds(pl.multiple_of(me * rows, rows), rows)])
+
+    for d in range(1, chan_count):
+        step_copy(d).wait()
+        source = lax.rem(me + chan_count - d, chan_count)
+        steps_order[source] = order_steps(steps_in[source])
+
+    def prepare(t, _):
+        prepare_head(t // heads, t % heads)
+        return 0
+
+    lax.fori_loop(0, chan_count * heads, prepare, 0)
 
     def own_head(head, _):
         state_head(me, head)
@@ -241,10 +270,7 @@
 
     lax.fori_loop(0, heads, own_head, 0)
     for d in range(1, chan_count):
-        step_copy(d).wait()
         carry_copy(d).wait()
-        source = lax.rem(me + chan_count - d, chan_count)
-        steps_order[source] = order_steps(steps_in[source])
 
     def arrive(t, _):
         s = t // (chan_count - 1)
@@ -264,21 +290,30 @@
     for j in range(run):
         sums_plain[pl.ds(j, ROWS, stride=run), :] = sums[j * ROWS:(j + 1) * ROWS, :]
     mean = jnp.sum(sums_plain[...], axis=1, keepdims=True) * (1.0 / gate.shape[1])
-    factor = jnp.broadcast_to(lax.rsqrt(mean + norm_epsilon), sums_plain.shape)
-
-    def finish(head, _):
-        cols = pl.ds(pl.multiple_of(head * LANES, LANES), LANES)
-        gain = gain_ref[pl.ds(head, 1), :]
-        out_ref[:, cols] = (gated_all[head] * factor * gain).astype(out_ref.dtype)
-        return 0
-
-    lax.fori_loop(0, gate.shape[1] // LANES, finish, 0)
+    factor_ref[...] = jnp.broadcast_to(lax.rsqrt(mean + norm_epsilon), factor_ref.shape)
 
     def sent(t, _):
         x_copy(t // (chan_count - 1), t % (chan_count - 1) + 1).wait_send()
         return 0
 
     lax.fori_loop(0, CHUNKS * (chan_count - 1), sent, 0)
+
+
+def scale_kernel(gated_ref, factor_ref, out_hbm, staged, sems):
+    heads, rows, _ = gated_ref.shape
+    part = heads // FINISH
+    copies = []
+    for piece in range(FINISH):
+        for inner in range(part):
+            head = piece * part + inner
+            value = gated_ref[head] * factor_ref[...]
+            staged[:, head * LANES:(head + 1) * LANES] = value.astype(staged.dtype)
+        cols = pl.ds(piece * part * LANES, part * LANES)
+        copy = pltpu.make_async_copy(staged.at[:, cols], out_hbm.at[:, cols], sems.at[piece])
+        copy.start()
+        copies.append(copy)
+    for copy in copies:
+        copy.wait()
 
 
 def per_device(tm_count, chan_count, inputs, gate_logits, step_sizes, decay_rates, skip_gain, norm_gain):
@@ -287,15 +322,17 @@
     heads = channels // LANES
     f32, bf16 = jnp.float32, jnp.bfloat16
     vmem = pl.BlockSpec(memory_space=pltpu.VMEM)
-    hbm = pl.BlockSpec(memory_space=pl.ANY)
+    hbm = pl.BlockSpec(memory_space=pltpu.HBM)
     dma = pltpu.SemaphoreType.DMA
-    return pl.pallas_call(
+    gated, factor = pl.pallas_call(
         functools.partial(kernel, tm_count=tm_count, chan_count=chan_count),
-        out_shape=jax.ShapeDtypeStruct((rows, width), bf16),
+        out_shape=(
+            pltpu.VMEM((width // LANES, rows, LANES), f32),
+            pltpu.VMEM((rows, LANES), f32),
+        ),
         in_specs=[hbm, hbm, vmem, vmem, vmem, vmem],
-        out_specs=vmem,
+        out_specs=(vmem, vmem),
         scratch_shapes=[
-            pltpu.VMEM((width // LANES, rows, LANES), f32),
             pltpu.VMEM((tokens, channels), bf16),
             pltpu.VMEM((rows, width), bf16),
             pltpu.VMEM((chan_count, rows, channels), bf16),
@@ -311,6 +348,7 @@
             pltpu.VMEM((chan_count, 1, channels), f32),
             pltpu.VMEM((rows, LANES), f32),
             pltpu.VMEM((rows, LANES), f32),
+            *[pltpu.VMEM((width // LANES, rows, LANES), f32)] * 4,
             dma((3,)),
             dma((CHUNKS, chan_count)),
             dma((CHUNKS, chan_count)),
@@ -322,11 +360,22 @@
             dma((chan_count,)),
         ],
         compiler_params=pltpu.CompilerParams(
-            collective_id=0, has_side_effects=True, vmem_limit_bytes=56 * 1024 * 1024
+            collective_id=0, has_side_effects=True, vmem_limit_bytes=58 * 1024 * 1024
         ),
     )(
         inputs, gate_logits, step_sizes.T,
         decay_rates.reshape(-1, LANES), skip_gain.reshape(-1, LANES), norm_gain.reshape(-1, LANES),
+    )
+    return pl.pallas_call(
+        scale_kernel,
+        out_shape=jax.ShapeDtypeStruct((rows, width), bf16),
+        in_specs=[vmem, vmem],
+        out_specs=hbm,
+        scratch_shapes=[pltpu.VMEM((rows, width), bf16), dma((FINISH,))],
+        compiler_params=pltpu.CompilerParams(vmem_limit_bytes=16 * 1024 * 1024),
+    )(
+        pltpu.with_memory_space_constraint(gated, pltpu.VMEM),
+        pltpu.with_memory_space_constraint(factor, pltpu.VMEM),
     )
 
 

time: 63.8 us -> 56.4 us (0.88)
  Pallas kernels: 60.5 us -> 56.2 us
  local copies, waits for them, and re-layouts: 3.1 us -> 0 us
    pallas_call x1, Pallas kernels: 60.5 us -> 54.8 us  [per_device(): pl.pallas_call(functools.partial(kernel, tm_count=tm_count, chan_count=ch...]
    unnamed x1 -> x0, local copies, waits for them, and re-layouts: 3.1 us -> none
    pallas_call x0 -> x1, Pallas kernels: none -> 1.44 us  [per_device(): pl.pallas_call(scale_kernel, out_shape=jax.ShapeDtypeStruct((rows, width)...]
where the time goes in v2:
time: 56.4 us; the launch traced here: 56.2 us
  Pallas kernels  56.2 us (100%)
    pallas_call x1, Pallas kernels, per_device(): pl.pallas_call(functools.partial(kernel, tm_count=tm_count, chan_count=ch...  54.8 us
    pallas_call x1, Pallas kernels, per_device(): pl.pallas_call(scale_kernel, out_shape=jax.ShapeDtypeStruct((rows, width)...  1.44 us

profile of v2, /device:TPU:0, one launch (start us, length us, event | category | flops | bytes accessed | tf_op | source)
XLA Modules:
  0.0 56.2 jit_solution(7099585095356734977)
XLA Ops:
  0.0 54.8 %shard_map.64 = (f32[64,128,128]{2,1,0:T(8,128)S(1)}, f32[128,128]{1,0:T(8,128)S(1)}) custom-call(bf16[512,2048]{1,0:T(8,128)(2,1)} %x_hbm.1, bf16[128,8192]{1,0:T(8,128)(2,1)} %gate_hbm.1, bf16[16,512]{1,0:T(8,128)(2,1)} %bitcast.7, f32[64,128]{1,0:T(8,128)} %bitcast.4, f32[64,128]{1,0:T(8,128)} %bitcast.5, f32[64,128]{1,0:T(8,128)} %bitcast.6), custom_call_target="tpu_custom_call" | custom-call | tf_op jit(solution)/shard_map/pallas_call | solution.py:327
  54.8 1.4 %shard_map.65 = bf16[128,8192]{1,0:T(8,128)(2,1)} custom-call(f32[64,128,128]{2,1,0:T(8,128)S(1)} %get-tuple-element.7.gated_ref, f32[128,128]{1,0:T(8,128)S(1)} %get-tuple-element.8.factor_ref), custom_call_target="tpu_custom_call" | custom-call | tf_op jit(solution)/shard_map/pallas_call | solution.py:369

commit v3 on v2

--- a/solution.py
+++ b/solution.py
@@ -37,6 +37,14 @@
     kept = jnp.where(twice < 0.0625, series, 1.0 - decay * decay)
     scale = kept * lax.rsqrt(jnp.maximum(kept, 1e-37))
     return decay, scale
+
+
+def upper(index, r):
+    return lax.rem(index // (1 << r), 2)
+
+
+def partner(index, r):
+    return index + (1 << r) * (1 - 2 * upper(index, r))
 
 
 def across_rows(prod, state):
@@ -58,6 +66,7 @@
     tot_prod, tot_state, block_out, block_in, carry_out, carry_in, sums, sums_plain,
     decays, scales, prods, silus,
     load_sem, x_send, x_recv, step_send, step_recv, block_send, block_recv, carry_send, carry_recv,
+    from_left, from_right,
     *, tm_count, chan_count,
 ):
     me_tm = lax.axis_index("tm")
@@ -74,18 +83,16 @@
     load_gate = pltpu.make_async_copy(gate_hbm, gate, load_sem.at[2])
     load_x.start()
     barrier = pltpu.get_barrier_semaphore()
-    for d in range(1, chan_count):
-        pl.semaphore_signal(
-            barrier, 1, device_id={"chan": lax.rem(me + d, chan_count)}, device_id_type=MESH
-        )
-
-    def greet(k, _):
-        pl.semaphore_signal(
-            barrier, 1, device_id={"tm": lax.rem(me_tm + k, tm_count)}, device_id_type=MESH
-        )
-        return 0
-
-    lax.fori_loop(1, tm_count, greet, 0)
+    rounds = (tm_count - 1).bit_length()
+    has_left, has_right = me >= 1, me + 1 < chan_count
+
+    def greet(peer):
+        pl.semaphore_signal(barrier, 1, device_id={"chan": peer}, device_id_type=MESH)
+
+    pl.when(has_left)(lambda: greet(me - 1))
+    pl.when(has_right)(lambda: greet(me + 1))
+    for r in range(rounds):
+        pl.semaphore_signal(barrier, 1, device_id={"tm": partner(me_tm, r)}, device_id_type=MESH)
     load_own.start()
     load_gate.start()
 
@@ -127,19 +134,34 @@
             device_id={"chan": peer}, device_id_type=MESH,
         )
 
-    def block_copy(k):
+    def block_copy(r):
         return pltpu.make_async_remote_copy(
-            src_ref=block_out, dst_ref=block_in.at[me_tm],
-            send_sem=block_send.at[k], recv_sem=block_recv.at[k],
-            device_id={"tm": lax.rem(me_tm + k, tm_count)}, device_id_type=MESH,
+            src_ref=block_out.at[r], dst_ref=block_in.at[r],
+            send_sem=block_send.at[r], recv_sem=block_recv.at[r],
+            device_id={"tm": partner(me_tm, r)}, device_id_type=MESH,
         )
 
     load_x.wait()
-    pl.semaphore_wait(barrier, tm_count - 1 + chan_count - 1)
-    for d in range(1, chan_count):
+    pl.semaphore_wait(barrier, rounds + has_left.astype(jnp.int32) + has_right.astype(jnp.int32))
+
+    def begin(d):
         x_copy(0, d).start()
-    for d in range(1, chan_count):
         step_copy(d).start()
+
+    def tell(sem, peer):
+        pl.semaphore_signal(sem, 1, device_id={"chan": peer}, device_id_type=MESH)
+
+    for far in range(1, chan_count):
+        right_is, left_is = me + far < chan_count, me >= far
+        if far > 1:
+            pl.when(has_right & (me + 1 >= far))(functools.partial(tell, from_left.at[far], me + 1))
+            pl.when(has_left & (me - 1 + far < chan_count))(
+                functools.partial(tell, from_right.at[far], me - 1)
+            )
+            pl.when(left_is)(lambda: pl.semaphore_wait(from_left.at[far], 1))
+            pl.when(right_is)(lambda: pl.semaphore_wait(from_right.at[far], 1))
+        pl.when(right_is)(functools.partial(begin, far))
+        pl.when(left_is)(functools.partial(begin, chan_count - far))
     for s in range(1, EARLY):
         for d in range(1, chan_count):
             x_copy(s, d).start()
@@ -168,33 +190,31 @@
             tot_state[i, :, cols] = last_state
             block_state = last_prod * block_state + last_state
             block_prod = block_prod * last_prod
-        block_out[0, :, cols] = block_prod
-        block_out[1, :, cols] = block_state
+        block_out[0, 0, :, cols] = block_prod
+        block_out[0, 1, :, cols] = block_state
         return 0
 
     lax.fori_loop(0, heads, total_head, 0)
 
-    def send_block(k, _):
-        block_copy(k).start()
-        return 0
-
-    lax.fori_loop(1, tm_count, send_block, 0)
-    block_in[me_tm] = block_out[...]
-    load_own.wait()
-    load_gate.wait()
-    sums[...] = jnp.zeros_like(sums)
-
-    def take_block(k, _):
-        block_copy(k).wait()
-        return 0
-
-    lax.fori_loop(1, tm_count, take_block, 0)
-
-    def fold(k, carried):
-        new = block_in[k, 0] * carried + block_in[k, 1]
-        return jnp.where(k < me_tm, new, carried)
-
-    carried = lax.fori_loop(0, tm_count, fold, jnp.zeros((1, channels), jnp.float32))
+    before_prod = jnp.ones((1, channels), jnp.float32)
+    carried = jnp.zeros((1, channels), jnp.float32)
+    for r in range(rounds):
+        block_copy(r).start()
+        if r == 0:
+            load_own.wait()
+            load_gate.wait()
+            sums[...] = jnp.zeros_like(sums)
+        block_copy(r).wait()
+        their_prod, their_state = block_in[r, 0], block_in[r, 1]
+        our_prod, our_state = block_out[r, 0], block_out[r, 1]
+        late = upper(me_tm, r) == 1
+        carried = jnp.where(late, before_prod * their_state + carried, carried)
+        before_prod = jnp.where(late, before_prod * their_prod, before_prod)
+        if r + 1 < rounds:
+            block_out[r + 1, 0] = our_prod * their_prod
+            block_out[r + 1, 1] = jnp.where(
+                late, our_prod * their_state + our_state, their_prod * our_state + their_state
+            )
     for i in range(chan_count):
         carry_out[i] = carried
         carried = tot_prod[i] * carried + tot_state[i]
@@ -320,6 +340,8 @@
     tokens, channels = inputs.shape
     rows, width = gate_logits.shape
     heads = channels // LANES
+    rounds = (tm_count - 1).bit_length()
+    assert tm_count == 1 << rounds
     f32, bf16 = jnp.float32, jnp.bfloat16
     vmem = pl.BlockSpec(memory_space=pltpu.VMEM)
     hbm = pl.BlockSpec(memory_space=pltpu.HBM)
@@ -342,8 +364,8 @@
             pltpu.VMEM((chan_count, rows, heads), bf16),
             pltpu.VMEM((chan_count, 1, channels), f32),
             pltpu.VMEM((chan_count, 1, channels), f32),
-            pltpu.VMEM((2, 1, channels), f32),
-            pltpu.VMEM((tm_count, 2, 1, channels), f32),
+            pltpu.VMEM((rounds, 2, 1, channels), f32),
+            pltpu.VMEM((rounds, 2, 1, channels), f32),
             pltpu.VMEM((chan_count, 1, channels), f32),
             pltpu.VMEM((chan_count, 1, channels), f32),
             pltpu.VMEM((rows, LANES), f32),
@@ -354,10 +376,12 @@
             dma((CHUNKS, chan_count)),
             dma((chan_count,)),
             dma((chan_count,)),
-            dma((tm_count,)),
-            dma((tm_count,)),
+            dma((rounds,)),
+            dma((rounds,)),
             dma((chan_count,)),
             dma((chan_count,)),
+            pltpu.SemaphoreType.REGULAR((chan_count,)),
+            pltpu.SemaphoreType.REGULAR((chan_count,)),
         ],
         compiler_params=pltpu.CompilerParams(
             collective_id=0, has_side_effects=True, vmem_limit_bytes=58 * 1024 * 1024

time: 56.4 us -> 55.5 us (0.984)
  Pallas kernels: 56.2 us -> 55.4 us
    pallas_call x1, Pallas kernels: 54.8 us -> 53.9 us  [per_device(): pl.pallas_call(functools.partial(kernel, tm_count=tm_count, chan_count=ch...]
where the time goes in v3:
time: 55.5 us; the launch traced here: 55.4 us
  Pallas kernels  55.4 us (100%)
    pallas_call x1, Pallas kernels, per_device(): pl.pallas_call(functools.partial(kernel, tm_count=tm_count, chan_count=ch...  53.9 us
    pallas_call x1, Pallas kernels, per_device(): pl.pallas_call(scale_kernel, out_shape=jax.ShapeDtypeStruct((rows, width)...  1.44 us

profile of v3, /device:TPU:0, one launch (start us, length us, event | category | flops | bytes accessed | tf_op | source)
XLA Modules:
  0.0 55.4 jit_solution(17325905108760417793)
XLA Ops:
  0.0 53.9 %shard_map.64 = (f32[64,128,128]{2,1,0:T(8,128)S(1)}, f32[128,128]{1,0:T(8,128)S(1)}) custom-call(bf16[512,2048]{1,0:T(8,128)(2,1)} %x_hbm.1, bf16[128,8192]{1,0:T(8,128)(2,1)} %gate_hbm.1, bf16[16,512]{1,0:T(8,128)(2,1)} %bitcast.7, f32[64,128]{1,0:T(8,128)} %bitcast.4, f32[64,128]{1,0:T(8,128)} %bitcast.5, f32[64,128]{1,0:T(8,128)} %bitcast.6), custom_call_target="tpu_custom_call" | custom-call | tf_op jit(solution)/shard_map/pallas_call | solution.py:349
  53.9 1.4 %shard_map.65 = bf16[128,8192]{1,0:T(8,128)(2,1)} custom-call(f32[64,128,128]{2,1,0:T(8,128)S(1)} %get-tuple-element.7.gated_ref, f32[128,128]{1,0:T(8,128)S(1)} %get-tuple-element.8.factor_ref), custom_call_target="tpu_custom_call" | custom-call | tf_op jit(solution)/shard_map/pallas_call | solution.py:393
